TPU v7x, 32 devices: a whole 2x2x4 slice. The times are simulated.
32 devices in a mesh: seq: 4 (over z), grp: 8 (over y, x, core).
Axes of the slice: x: 2, y: 2, z: 4, core: 2. Of those that a mesh axis runs over, the one named last changes fastest.
Arguments:
- hidden_in: bfloat16 [8, 2048, 1024], P('grp', 'seq'), may hold values from -64 to 64, as said below
- lengths: int32 [8], P('grp'), may hold values from 256 to 2048
- project_weight: bfloat16 [1024, 3072], replicated, may hold values from -0.1875 to 0.1875
- output_weight: bfloat16 [1024, 1024], replicated, may hold values from -0.1875 to 0.1875
- first_gain: float32 [1024], replicated, may hold values from 0.5 to 1.5
- first_shift: float32 [1024], replicated, may hold values from -3 to 3
- up_weight: bfloat16 [1024, 4096], P('grp'), may hold values from -0.1875 to 0.1875
- down_weight: bfloat16 [1024, 4096], P('grp'), may hold values from -0.09375 to 0.09375
- second_gain: float32 [1024], replicated, may hold values from 0.5 to 1.5
- second_shift: float32 [1024], replicated, may hold values from -3 to 3
- queries: float32 [64, 1024], P('grp'), may hold values from -6 to 6
- positive: int32 [64], P('grp'), may hold values from 0 to 7
Outputs:
- hidden_out: bfloat16 [8, 2048, 1024], P('grp', 'seq')
- embeddings: float32 [8, 1024], P('grp')
- query_loss: float32 [64], P('grp')
Inputs may be any that keep to these rules, and one draw needn't show every extreme that they name: `hidden_in`: activations.
All inputs are finite; a program needn't handle non-finite values.
Results may differ from a plain program's by a relative error of at most 0.0076.
Values may be sent and summed in bfloat16 or wider, within the bound.
A program may use at most 192 MiB of HBM per device.

v0:
```python
import math
import jax
import jax.numpy as jnp
from jax import lax
from jax.sharding import PartitionSpec as P

HEAD_DIM = 64


def layer_norm(values, gain, shift):
    average = jnp.mean(values, axis=-1, keepdims=True)
    centred = values - average
    variance = jnp.mean(centred * centred, axis=-1, keepdims=True)
    return centred * lax.rsqrt(variance + 1e-05) * gain + shift


def attend_local(gathered, length):
    seq_len = gathered.shape[0]
    local_width = gathered.shape[2]
    head_count = local_width // HEAD_DIM
    block = min(1024, seq_len)
    query_all = gathered[:, 0, :].reshape(seq_len, head_count, HEAD_DIM)
    key_all = gathered[:, 1, :].reshape(seq_len, head_count, HEAD_DIM)
    value_all = gathered[:, 2, :].reshape(seq_len, head_count, HEAD_DIM)
    key_valid = jnp.arange(seq_len, dtype=jnp.int32) < length
    scale = 1.0 / math.sqrt(HEAD_DIM)

    def one_block(index):
        query_rows = lax.dynamic_slice_in_dim(query_all, index * block, block, 0)
        scores = (
            jnp.einsum("qhd,khd->hqk", query_rows, key_all, preferred_element_type=jnp.float32)
            * scale
        )
        scores = jnp.where(key_valid[None, None, :], scores, -jnp.inf)
        highest = jnp.max(scores, axis=-1, keepdims=True)
        expo = jnp.exp(scores - highest)
        probs = (expo / jnp.sum(expo, axis=-1, keepdims=True)).astype(jnp.bfloat16)
        result = jnp.einsum("hqk,khd->qhd", probs, value_all, preferred_element_type=jnp.float32)
        return result.astype(jnp.bfloat16).reshape(block, local_width)

    blocks = lax.map(one_block, jnp.arange(seq_len // block, dtype=jnp.int32))
    return blocks.reshape(seq_len, local_width)


def group_weights(up_part, down_part):
    return (
        lax.all_gather(up_part, "grp", axis=0, tiled=True),
        lax.all_gather(down_part, "grp", axis=0, tiled=True),
    )


def expand_inner(rows_in, up_full):
    return jax.nn.gelu(
        jnp.dot(rows_in, up_full, preferred_element_type=jnp.float32), approximate=False
    ).astype(jnp.bfloat16)


def contract_down(inner_rows, down_full):
    return lax.dot_general(
        inner_rows, down_full, (((1,), (1,)), ((), ())), preferred_element_type=jnp.float32
    )


def body(
    hidden_in,
    lengths,
    project_weight,
    output_weight,
    first_gain,
    first_shift,
    up_weight,
    down_weight,
    second_gain,
    second_shift,
    queries,
    positive,
):
    tokens = hidden_in[0]
    tok_rows = tokens.shape[0]
    width = tokens.shape[1]
    rank = lax.axis_index("seq")
    length = lengths[0]
    projected = jnp.dot(tokens, project_weight, preferred_element_type=jnp.float32).astype(
        jnp.bfloat16
    )
    projected = projected.reshape(tok_rows, 3, width)
    gathered = lax.all_to_all(projected, "seq", split_axis=2, concat_axis=0, tiled=True)
    attended = attend_local(gathered, length)
    returned = lax.all_to_all(attended, "seq", split_axis=0, concat_axis=1, tiled=True)
    mixed = jnp.dot(returned, output_weight, preferred_element_type=jnp.float32)
    mixed = mixed + tokens.astype(jnp.float32)
    normed = layer_norm(mixed, first_gain, first_shift).astype(jnp.bfloat16)
    up_full, down_full = group_weights(up_weight, down_weight)
    inner = expand_inner(normed, up_full)
    outer = contract_down(inner, down_full)
    final = layer_norm(outer + normed.astype(jnp.float32), second_gain, second_shift)
    position = rank * tok_rows + jnp.arange(tok_rows, dtype=jnp.int32)
    valid = (position < length).astype(jnp.float32)
    local_total = jnp.sum(final * valid[:, None], axis=0)
    passage_total = lax.psum(local_total, "seq")
    pooled = passage_total / length.astype(jnp.float32)
    embedding = pooled / jnp.sqrt(jnp.sum(pooled * pooled) + 1e-06)
    short_passages = lax.all_gather(
        embedding.astype(jnp.bfloat16)[None, :], "grp", axis=0, tiled=True
    )
    short_queries = (
        queries / jnp.sqrt(jnp.sum(queries * queries, axis=-1, keepdims=True) + 1e-06)
    ).astype(jnp.bfloat16)
    logits = 20.0 * jnp.dot(short_queries, short_passages.T, preferred_element_type=jnp.float32)
    passage_ids = jnp.arange(short_passages.shape[0], dtype=jnp.int32)
    chosen = positive[:, None] == passage_ids[None, :]
    picked = jnp.sum(jnp.where(chosen, logits, 0.0), axis=1)
    query_loss = jnp.log(jnp.sum(jnp.exp(logits), axis=1)) - picked
    return (final.astype(jnp.bfloat16)[None], embedding[None, :], query_loss)


def solution(mesh):
    in_specs = (
        P("grp", "seq", None),
        P("grp"),
        P(),
        P(),
        P(),
        P(),
        P("grp", None),
        P("grp", None),
        P(),
        P(),
        P("grp", None),
        P("grp"),
    )
    out_specs = (P("grp", "seq", None), P("grp", None), P("grp"))
    return jax.shard_map(body, mesh=mesh, in_specs=in_specs, out_specs=out_specs, check_vma=False)
```

profile of v0, /device:TPU:0, one launch (start us, length us, event | category | flops | bytes accessed | tf_op | source)
XLA Modules:
  0.0 300.3 jit_solution(4461810352505724888)
XLA Ops:
  7.2 0.0 copy-start
  7.2 0.0 all-gather.4.cloned.1.call-start
  7.2 0.7 all-gather.4.cloned.1.call-update
  7.9 0.0 all-gather.6.cloned.1.call-start
  8.0 0.7 all-gather.6.cloned.1.call-update
  8.7 8.2 %convolution_convert_fusion = bf16[512,3072]{1,0:T(8,128)(2,1)} fusion(bf16[1024,3072]{1,0:T(8,128)(2,1)} %param.16, bf16[1,512,1024]{2,1,0:T(8,128)(2,1)} %param.14), kind=kOutput, calls=%fused_computation.44 | convolution fusion | flops 3222798336 | bytes 10485760 | tf_op jit(solution)/shard_map/dot_general | solution.py:83
  16.9 4.8 %copy.33 = bf16[512,3072]{0,1:T(8,128)(2,1)} copy(bf16[512,3072]{1,0:T(8,128)(2,1)} %convolution_convert_fusion) | data formatting | bytes 6291456 | tf_op jit(solution)/shard_map/convert_element_type | solution.py:83
  21.7 6.6 %copy.34 = bf16[512,3,1024]{0,1,2:T(4,128)(2,1)} copy(bf16[512,3,1024]{0,2,1:T(8,128)(2,1)} %bitcast.51) | data formatting | bytes 6291456 | tf_op jit(solution)/shard_map/reshape | solution.py:86
  28.3 6.3 %all-to-all-start = ((bf16[512,3,1024]{0,1,2:T(4,128)(2,1)}), bf16[512,3,1024]{0,1,2:T(4,128)(2,1)}, u32[]{:S(2)}, u32[]{:S(2)}) async-start(bf16[512,3,1024]{0,1,2:T(4,128)(2,1)} %copy.34), calls=%async_computation | async-start | bytes 8388608 | tf_op jit(solution)/shard_map/all_to_all | solution.py:87
  34.6 93.4 %all-to-all-done = bf16[512,3,1024]{0,1,2:T(4,128)(2,1)} async-done(((bf16[512,3,1024]{0,1,2:T(4,128)(2,1)}), bf16[512,3,1024]{0,1,2:T(4,128)(2,1)}, u32[]{:S(2)}, u32[]{:S(2)}) %all-to-all-start) | async-done | bytes 3145760 | tf_op jit(solution)/shard_map/all_to_all | solution.py:87
  128.0 4.7 %copy.35 = bf16[512,3,1024]{0,2,1:T(8,128)(2,1)} copy(bf16[512,3,1024]{0,1,2:T(4,128)(2,1)} %all-to-all-done) | data formatting | bytes 6291456 | tf_op jit(solution)/shard_map/all_to_all | solution.py:87
  132.7 4.7 %copy.36 = bf16[4,512,3,256]{3,1,0,2:T(8,128)(2,1)} copy(bf16[4,512,3,256]{1,3,0,2:T(8,128)(2,1)} %bitcast.52) | data formatting | bytes 6291456 | tf_op jit(solution)/shard_map/all_to_all | solution.py:87
  137.3 3.4 %fusion.97 = (bf16[2048,1,256]{2,0,1:T(8,128)(2,1)S(1)}, bf16[2048,1,256]{2,0,1:T(8,128)(2,1)}, bf16[2048,1,256]{2,0,1:T(8,128)(2,1)}) fusion(bf16[2048,3,256]{2,0,1:T(8,128)(2,1)} %bitcast.53), kind=kLoop, calls=%fused_computation.105 | loop fusion | bytes 6291456 | tf_op jit(solution)/shard_map/slice | solution.py:24
  140.8 2.3 copy.37
  143.1 2.3 copy.38
  145.3 1.4 copy.39
  146.8 0.0 copy-start.2
  146.8 52.2 %while.11 = (s32[]{:T(128)}, bf16[2,1024,256]{2,1,0:T(8,128)(2,1)}, s32[2]{0:T(128)S(1)}, bf16[2048,4,64]{0,2,1:T(8,128)(2,1)}, bf16[2048,4,64]{0,2,1:T(8,128)(2...) while((s32[]{:T(128)}, bf16[2,1024,256]{2,1,0:T(8,128)(2,1)}, ...), condition=%wide.region_3.4_spmd.clone, body=%wide.region_0.3_spmd.clone.sunk | while | flops 3296995328 | bytes 6855347 | solution.py:41
  146.8 0.6 dynamic_slice.31
  148.0 0.7 iota_compare_fusion.3
  148.7 11.0 %fusion.127 = f32[4,1024]{1,0:T(4,128)S(1)} fusion(pred[2048]{0:T(1024)(128)(4,1)S(1)} %iota_compare_fusion.3, bf16[2048,4,64]{0,2,1:T(8,128)(2,1)} %get-tuple-element.161, bf16[2048,4,64]{0,2,1:T(8,128)(2,1)} %get-tuple-element.160, s32[]{:T(128)S(6)} %select_n.42), kind=kOutput, calls=%fused_computation.104.clone.1 | convolution fusion | flops 1107298304 | bytes 1591300 | tf_op jit(solution)/shard_map/while/body/eval_jaxpr/sub | solution.py:36
  159.7 12.2 %fusion.128 = bf16[4,1024,64]{1,2,0:T(8,128)(2,1)S(1)} fusion(bf16[2048,4,64]{0,2,1:T(8,128)(2,1)} %get-tuple-element.162, f32[4,1024]{1,0:T(4,128)S(1)} %fusion.127, pred[2048]{0:T(1024)(128)(4,1)S(1)} %iota_compare_fusion.3, bf16[2048,4,64]{0,2,1:T(8,128)(2,1)} %get-tuple-element.161, bf16[2048,4,64]{0,2,1:T(8,128)(2,1)} %get-tuple-element.160, ...), kind=kOutput, calls=%fused_computation.11.clone.1 | convolution fusion | flops 2189694976 | bytes 3164164 | tf_op jit(solution)/shard_map/while/body/eval_jaxpr/hqk,khd->qhd/dot_general | solution.py:38
  171.8 0.2 copy.45
  172.0 0.8 constant_dynamic-update-slice_fusion.2
  172.9 0.6 dynamic_slice.31
  174.1 0.7 iota_compare_fusion.3
  174.8 11.0 %fusion.127 = f32[4,1024]{1,0:T(4,128)S(1)} fusion(pred[2048]{0:T(1024)(128)(4,1)S(1)} %iota_compare_fusion.3, bf16[2048,4,64]{0,2,1:T(8,128)(2,1)} %get-tuple-element.161, bf16[2048,4,64]{0,2,1:T(8,128)(2,1)} %get-tuple-element.160, s32[]{:T(128)S(6)} %select_n.42), kind=kOutput, calls=%fused_computation.104.clone.1 | convolution fusion | flops 1107298304 | bytes 1591300 | tf_op jit(solution)/shard_map/while/body/eval_jaxpr/sub | solution.py:36
  185.8 12.2 %fusion.128 = bf16[4,1024,64]{1,2,0:T(8,128)(2,1)S(1)} fusion(bf16[2048,4,64]{0,2,1:T(8,128)(2,1)} %get-tuple-element.162, f32[4,1024]{1,0:T(4,128)S(1)} %fusion.127, pred[2048]{0:T(1024)(128)(4,1)S(1)} %iota_compare_fusion.3, bf16[2048,4,64]{0,2,1:T(8,128)(2,1)} %get-tuple-element.161, bf16[2048,4,64]{0,2,1:T(8,128)(2,1)} %get-tuple-element.160, ...), kind=kOutput, calls=%fused_computation.11.clone.1 | convolution fusion | flops 2189694976 | bytes 3164164 | tf_op jit(solution)/shard_map/while/body/eval_jaxpr/hqk,khd->qhd/dot_general | solution.py:38
  197.9 0.2 copy.45
  198.1 0.8 constant_dynamic-update-slice_fusion.2
  199.0 0.0 copy-start.5
  199.0 0.0 copy-start.6
  199.0 3.6 %all-to-all-start.1 = ((bf16[4,512,256]{2,1,0:T(8,128)(2,1)}), bf16[4,512,256]{2,1,0:T(8,128)(2,1)S(1)}, u32[]{:S(2)}, u32[]{:S(2)}) async-start(bf16[4,512,256]{2,1,0:T(8,128)(2,1)} %bitcast.59), calls=%async_computation.1 | async-start | bytes 2097152 | tf_op jit(solution)/shard_map/all_to_all | solution.py:89
  203.3 0.0 copy-done.2
  203.3 0.1 multiply_reduce_fusion.3
  203.4 24.3 %all-to-all-done.1 = bf16[4,512,256]{2,1,0:T(8,128)(2,1)S(1)} async-done(((bf16[4,512,256]{2,1,0:T(8,128)(2,1)}), bf16[4,512,256]{2,1,0:T(8,128)(2,1)S(1)}, u32[]{:S(2)}, u32[]{:S(2)}) %all-to-all-start.1) | async-done | bytes 1048608 | tf_op jit(solution)/shard_map/all_to_all | solution.py:89
  227.8 1.3 copy.41
  229.1 0.0 copy-done
  229.1 2.9 fusion.98
  232.0 0.0 copy-start.1
  232.0 1.3 copy-done.1
  233.3 0.3 multiply_reduce_fusion.2
  233.7 0.0 copy-start.3
  233.7 0.0 copy-start.4
  233.7 0.0 copy-start.7
  233.7 0.0 all-gather.4.cloned.1.call-done
  233.7 0.0 all-gather.6.cloned.1.call-done
  233.8 0.0 copy-done.5
  233.8 0.0 copy-done.6
  233.8 33.2 %fusion.99 = (f32[512]{0:T(512)S(1)}, f32[512,1024]{1,0:T(8,128)}) fusion(f32[1024]{0:T(1024)S(1)} %copy-done.5, f32[1024]{0:T(1024)S(1)} %copy-done.6, f32[512]{0:T(512)S(1)} %add_rsqrt_fusion.1, f32[512,1024]{1,0:T(8,128)} %copy-done.1, f32[512]{0:T(512)S(1)} %broadcast_multiply_fusion.1, bf16[1024,4096]{1,0:T(8,128)(2,1)} %all-gather.6.cloned.1.call-done, ...), kind=kOutput, calls=%fused_computation.107 | convolution fusion | flops 8733065216 | bytes 20985856 | tf_op jit(solution)/shard_map/dot_general | solution.py:59
  267.0 1.9 multiply_reduce_fusion.1
  268.9 0.0 copy-done.3
  268.9 0.0 copy-done.4
  268.9 3.1 %multiply_reduce_fusion = (f32[1024]{0:T(1024)S(1)}, bf16[1,512,1024]{2,1,0:T(8,128)(2,1)}) fusion(f32[512,1024]{1,0:T(8,128)} %get-tuple-element.91, f32[512]{0:T(512)S(1)} %fusion.59, f32[1024]{0:T(1024)S(1)} %copy-done.3, f32[1024]{0:T(1024)S(1)} %copy-done.4, f32[512]{0:T(512)S(1)} %add_rsqrt_fusion, f32[512]{0:T(512)S(1)} %broadcast_multiply_fusion), kind=kLoop, calls=%fused_computation.46 | loop fusion | flops 3668992 | bytes 3164160 | tf_op jit(solution)/shard_map/reduce_sum | solution.py:99
  272.0 9.8 %psum.7 = f32[1024]{0:T(1024)S(1)} all-reduce(f32[1024]{0:T(1024)S(1)} %get-tuple-element.86), channel_id=1, replica_groups=mesh['seq'=4,'grp'=8] {'seq'}, use_global_device_ids=true, to_apply=%region_9.10 | all-reduce | flops 1024 | bytes 8192 | tf_op jit(solution)/shard_map/psum | solution.py:100
  281.8 0.6 multiply_reduce_fusion.4
  283.1 0.6 fusion.91
  283.7 9.0 %all-gather = bf16[8192]{0:T(1024)(128)(2,1)S(1)} all-gather(bf16[1024]{0:T(1024)(128)(2,1)S(1)} %get-tuple-element.81), channel_id=2, replica_groups=mesh['seq'=4,'grp'=8] {'grp'}, dimensions={0}, use_global_device_ids=true | all-gather | bytes 18432 | tf_op jit(solution)/shard_map/all_gather | solution.py:103
  292.7 0.0 copy-done.7
  292.7 0.2 exponential_reduce_fusion
  292.9 0.5 log_subtract_fusion
  (9 shorter events, 0.1 us)
Async XLA Ops:
  7.2 221.9 %copy-start = (bf16[1024,1024]{1,0:T(8,128)(2,1)S(1)}, bf16[1024,1024]{1,0:T(8,128)(2,1)}, u32[]{:S(2)}) copy-start(bf16[1024,1024]{1,0:T(8,128)(2,1)} %param.17) | copy-start | bytes 6291460
  7.2 226.6 %all-gather.4.cloned.1.call-start = ((), (), s32[]{:S(2)}) async-start(), calls=%async_computation.2 | async-start | bytes 9437184 | tf_op jit(solution)/shard_map/all_gather | solution.py:47
  7.9 225.8 %all-gather.6.cloned.1.call-start = ((), (), s32[]{:S(2)}) async-start(), calls=%async_computation.3 | async-start | bytes 9437184 | tf_op jit(solution)/shard_map/all_gather | solution.py:48
  28.3 99.7 %all-to-all-start = ((bf16[512,3,1024]{0,1,2:T(4,128)(2,1)}), bf16[512,3,1024]{0,1,2:T(4,128)(2,1)}, u32[]{:S(2)}, u32[]{:S(2)}) async-start(bf16[512,3,1024]{0,1,2:T(4,128)(2,1)} %copy.34), calls=%async_computation | async-start | bytes 8388608 | tf_op jit(solution)/shard_map/all_to_all | solution.py:87
  146.8 56.5 %copy-start.2 = (f32[8,1024]{1,0:T(8,128)S(1)}, f32[8,1024]{1,0:T(8,128)}, u32[]{:S(2)}) copy-start(f32[8,1024]{1,0:T(8,128)} %param.24) | copy-start | bytes 98308
  199.0 34.8 %copy-start.5 = (f32[1024]{0:T(1024)S(1)}, f32[1024]{0:T(1024)}, u32[]{:S(2)}) copy-start(f32[1024]{0:T(1024)} %param.19) | copy-start | bytes 12292
  199.0 34.8 %copy-start.6 = (f32[1024]{0:T(1024)S(1)}, f32[1024]{0:T(1024)}, u32[]{:S(2)}) copy-start(f32[1024]{0:T(1024)} %param.18) | copy-start | bytes 12292
  199.0 28.8 %all-to-all-start.1 = ((bf16[4,512,256]{2,1,0:T(8,128)(2,1)}), bf16[4,512,256]{2,1,0:T(8,128)(2,1)S(1)}, u32[]{:S(2)}, u32[]{:S(2)}) async-start(bf16[4,512,256]{2,1,0:T(8,128)(2,1)} %bitcast.59), calls=%async_computation.1 | async-start | bytes 2097152 | tf_op jit(solution)/shard_map/all_to_all | solution.py:89
  232.0 1.4 copy-start.1
  233.7 35.3 %copy-start.3 = (f32[1024]{0:T(1024)S(1)}, f32[1024]{0:T(1024)}, u32[]{:S(2)}) copy-start(f32[1024]{0:T(1024)} %param.23) | copy-start | bytes 12292
  233.7 35.3 %copy-start.4 = (f32[1024]{0:T(1024)S(1)}, f32[1024]{0:T(1024)}, u32[]{:S(2)}) copy-start(f32[1024]{0:T(1024)} %param.22) | copy-start | bytes 12292
  233.7 59.0 %copy-start.7 = (s32[8]{0:T(128)S(1)}, s32[8]{0:T(128)}, u32[]{:S(2)}) copy-start(s32[8]{0:T(128)} %param.25) | copy-start | bytes 100
Sparse Core Ops, SparseCore 0:
  9.9 56.9 all-gather.3
  68.8 54.2 all-gather.5
where the time goes:
time: 301 us; the launch traced here: 300 us
  waiting for transfers between devices  119 us (40%)
  matrix products  90.8 us (30%)
  local copies, waits for them, and re-layouts  36.1 us (12%)
  blocking collectives  18.7 us (6%)
  between operations  15.5 us (5%)
  starting transfers between devices  10 us (3%)
  other arithmetic  8.57 us (3%)
    all_to_all x1, waiting for transfers between devices, body(): lax.all_to_all(projected, 'seq', split_axis=2, concat_axis=0, tiled=True)  93.4 us
    dot_general x1, matrix products, contract_down(): lax.dot_general(inner_rows, down_full, (((1,), (1,)), ((), ())), preferre...  33.2 us
    all_to_all x1, waiting for transfers between devices, body(): lax.all_to_all(attended, 'seq', split_axis=0, concat_axis=1, tiled=True)  24.3 us
    dot_general x2, matrix products, one_block(): jnp.einsum('hqk,khd->qhd', probs, value_all, preferred_element_type=jnp.f...  24.3 us
    sub x2, matrix products, one_block(): expo = jnp.exp(scores - highest)  22 us
    psum x1, blocking collectives, body(): passage_total = lax.psum(local_total, 'seq')  9.76 us
    all_to_all x2, local copies, waits for them, and re-layouts, body(): lax.all_to_all(projected, 'seq', split_axis=2, concat_axis=0, tiled=True)  9.34 us
    all_gather x1, blocking collectives, body(): lax.all_gather(embedding.astype(jnp.bfloat16)[None, :], 'grp', axis=0, ti...  8.97 us
  transfers between devices with their start and end apart: 4, of which 2 were waited for; matrix products, arithmetic and copies ran while one was open for 31% of the time, Pallas kernels for 0%

commit v1 on v0

--- a/solution.py
+++ b/solution.py
@@ -1,3 +1,4 @@
+import functools
 import math
 import jax
 import jax.numpy as jnp
@@ -5,6 +6,15 @@
 from jax.sharding import PartitionSpec as P
 
 HEAD_DIM = 64
+
+
+def move_records_all(load, dev_axis):
+    return jnp.concatenate(
+        lax.all_to_all(jnp.stack(jnp.split(load, lax.axis_size(dev_axis), 2), 0), dev_axis, 0, 0), 0
+    )
+
+
+track_the_widths = functools.partial(move_records_all, dev_axis="seq")
 
 
 def layer_norm(values, gain, shift):
@@ -84,7 +94,7 @@
         jnp.bfloat16
     )
     projected = projected.reshape(tok_rows, 3, width)
-    gathered = lax.all_to_all(projected, "seq", split_axis=2, concat_axis=0, tiled=True)
+    gathered = track_the_widths(projected)
     attended = attend_local(gathered, length)
     returned = lax.all_to_all(attended, "seq", split_axis=0, concat_axis=1, tiled=True)
     mixed = jnp.dot(returned, output_weight, preferred_element_type=jnp.float32)

time: 301 us -> 271 us (0.900)
  waiting for transfers between devices: 119 us -> 96.6 us
  local copies, waits for them, and re-layouts: 36.1 us -> 27.1 us
    all_to_all x1, waiting for transfers between devices: 93.4 us -> 70.9 us  [move_records_all(): lax.all_to_all(jnp.stack(jnp.split(load, lax.axis_size(dev_axis), 2), 0),...]
    reshape x1 -> x0, local copies, waits for them, and re-layouts: 6.65 us -> none  [body(): projected = projected.reshape(tok_rows, 3, width)]
    all_to_all x2 -> x1, local copies, waits for them, and re-layouts: 9.34 us -> 4.69 us  [move_records_all(): lax.all_to_all(jnp.stack(jnp.split(load, lax.axis_size(dev_axis), 2), 0),...]
  transfers between devices with their start and end apart: 4 -> 4, of which waited for: 2 -> 2; matrix products, arithmetic and copies ran while one was open for 31% -> 32% of each run, Pallas kernels for 0% -> 0%
where the time goes in v1:
time: 271 us
  waiting for transfers between devices  96.6 us (36%)
  matrix products  90.8 us (34%)
  local copies, waits for them, and re-layouts  27.1 us (10%)
  blocking collectives  18.6 us (7%)
  between operations  15.5 us (6%)
  other arithmetic  10.4 us (4%)
  starting transfers between devices  10 us (4%)
    all_to_all x1, waiting for transfers between devices, move_records_all(): lax.all_to_all(jnp.stack(jnp.split(load, lax.axis_size(dev_axis), 2), 0),...  70.9 us
    dot_general x1, matrix products, contract_down(): lax.dot_general(inner_rows, down_full, (((1,), (1,)), ((), ())), preferre...  33.2 us
    dot_general x2, matrix products, one_block(): jnp.einsum('hqk,khd->qhd', probs, value_all, preferred_element_type=jnp.f...  24.3 us
    all_to_all x1, waiting for transfers between devices, body(): lax.all_to_all(attended, 'seq', split_axis=0, concat_axis=1, tiled=True)  24.3 us
    sub x2, matrix products, one_block(): expo = jnp.exp(scores - highest)  22 us
    psum x1, blocking collectives, body(): passage_total = lax.psum(local_total, 'seq')  9.76 us
    all_gather x1, blocking collectives, body(): lax.all_gather(embedding.astype(jnp.bfloat16)[None, :], 'grp', axis=0, ti...  8.89 us
    dot_general x1, matrix products, body(): jnp.dot(tokens, project_weight, preferred_element_type=jnp.float32)  8.21 us
  transfers between devices with their start and end apart: 4, of which 2 were waited for; matrix products, arithmetic and copies ran while one was open for 32% of the time, Pallas kernels for 0%

profile of v1, /device:TPU:0, one launch (start us, length us, event | category | flops | bytes accessed | tf_op | source)
XLA Modules:
  0.0 270.5 jit_solution(476706529264340565)
XLA Ops:
  7.2 0.0 copy-start
  7.2 0.0 all-gather.4.cloned.1.call-start
  7.2 0.7 all-gather.4.cloned.1.call-update
  7.9 0.0 all-gather.6.cloned.1.call-start
  8.0 0.7 all-gather.6.cloned.1.call-update
  8.7 8.2 %convolution_convert_fusion = bf16[512,3072]{1,0:T(8,128)(2,1)} fusion(bf16[1024,3072]{1,0:T(8,128)(2,1)} %param.16, bf16[1,512,1024]{2,1,0:T(8,128)(2,1)} %param.14), kind=kOutput, calls=%fused_computation.44 | convolution fusion | flops 3222798336 | bytes 10485760 | tf_op jit(solution)/shard_map/dot_general | solution.py:93
  16.9 4.8 %copy.35 = bf16[512,3072]{0,1:T(8,128)(2,1)} copy(bf16[512,3072]{1,0:T(8,128)(2,1)} %convolution_convert_fusion) | data formatting | bytes 6291456 | tf_op jit(solution)/shard_map/convert_element_type | solution.py:93
  21.7 2.1 slice_bitcast_fusion.3
  23.8 1.9 pad_maximum_fusion
  25.7 6.3 %all-to-all-start = ((bf16[4,512,3,256]{1,3,2,0:T(8,128)(2,1)}), bf16[4,512,3,256]{1,3,2,0:T(8,128)(2,1)}, u32[]{:S(2)}, u32[]{:S(2)}) async-start(bf16[4,512,3,256]{1,3,2,0:T(8,128)(2,1)} %pad_maximum_fusion), calls=%async_computation | async-start | bytes 6291456 | tf_op jit(solution)/shard_map/all_to_all | solution.py:13
  32.0 70.9 %all-to-all-done = bf16[4,512,3,256]{1,3,2,0:T(8,128)(2,1)} async-done(((bf16[4,512,3,256]{1,3,2,0:T(8,128)(2,1)}), bf16[4,512,3,256]{1,3,2,0:T(8,128)(2,1)}, u32[]{:S(2)}, u32[]{:S(2)}) %all-to-all-start) | async-done | bytes 3145760 | tf_op jit(solution)/shard_map/all_to_all | solution.py:13
  102.9 4.7 %copy.36 = bf16[4,512,3,256]{3,1,0,2:T(8,128)(2,1)} copy(bf16[4,512,3,256]{1,3,2,0:T(8,128)(2,1)} %all-to-all-done) | data formatting | bytes 6291456 | tf_op jit(solution)/shard_map/all_to_all | solution.py:13
  107.6 3.5 %fusion.97 = (bf16[2048,1,256]{2,0,1:T(8,128)(2,1)S(1)}, bf16[2048,1,256]{2,0,1:T(8,128)(2,1)}, bf16[2048,1,256]{2,0,1:T(8,128)(2,1)}) fusion(bf16[2048,3,256]{2,0,1:T(8,128)(2,1)} %bitcast.57), kind=kLoop, calls=%fused_computation.110 | loop fusion | bytes 6291456 | tf_op jit(solution)/shard_map/slice | solution.py:34
  111.0 2.3 copy.37
  113.3 2.3 copy.38
  115.6 1.4 copy.39
  117.1 0.0 copy-start.2
  117.1 52.2 %while.11 = (s32[]{:T(128)}, bf16[2,1024,256]{2,1,0:T(8,128)(2,1)}, s32[2]{0:T(128)S(1)}, bf16[2048,4,64]{0,2,1:T(8,128)(2,1)}, bf16[2048,4,64]{0,2,1:T(8,128)(2...) while((s32[]{:T(128)}, bf16[2,1024,256]{2,1,0:T(8,128)(2,1)}, ...), condition=%wide.region_3.4_spmd.clone, body=%wide.region_0.3_spmd.clone.sunk | while | flops 3296995328 | bytes 6855347 | solution.py:51
  117.1 0.6 dynamic_slice.31
  118.3 0.7 iota_compare_fusion.3
  119.0 11.0 %fusion.127 = f32[4,1024]{1,0:T(4,128)S(1)} fusion(pred[2048]{0:T(1024)(128)(4,1)S(1)} %iota_compare_fusion.3, bf16[2048,4,64]{0,2,1:T(8,128)(2,1)} %get-tuple-element.165, bf16[2048,4,64]{0,2,1:T(8,128)(2,1)} %get-tuple-element.164, s32[]{:T(128)S(6)} %select_n.42), kind=kOutput, calls=%fused_computation.109.clone.1 | convolution fusion | flops 1107298304 | bytes 1591300 | tf_op jit(solution)/shard_map/while/body/eval_jaxpr/sub | solution.py:46
  130.0 12.2 %fusion.128 = bf16[4,1024,64]{1,2,0:T(8,128)(2,1)S(1)} fusion(bf16[2048,4,64]{0,2,1:T(8,128)(2,1)} %get-tuple-element.166, f32[4,1024]{1,0:T(4,128)S(1)} %fusion.127, pred[2048]{0:T(1024)(128)(4,1)S(1)} %iota_compare_fusion.3, bf16[2048,4,64]{0,2,1:T(8,128)(2,1)} %get-tuple-element.165, bf16[2048,4,64]{0,2,1:T(8,128)(2,1)} %get-tuple-element.164, ...), kind=kOutput, calls=%fused_computation.11.clone.1 | convolution fusion | flops 2189694976 | bytes 3164164 | tf_op jit(solution)/shard_map/while/body/eval_jaxpr/hqk,khd->qhd/dot_general | solution.py:48
  142.2 0.2 copy.45
  142.4 0.8 constant_dynamic-update-slice_fusion.2
  143.2 0.6 dynamic_slice.31
  144.4 0.7 iota_compare_fusion.3
  145.1 11.0 %fusion.127 = f32[4,1024]{1,0:T(4,128)S(1)} fusion(pred[2048]{0:T(1024)(128)(4,1)S(1)} %iota_compare_fusion.3, bf16[2048,4,64]{0,2,1:T(8,128)(2,1)} %get-tuple-element.165, bf16[2048,4,64]{0,2,1:T(8,128)(2,1)} %get-tuple-element.164, s32[]{:T(128)S(6)} %select_n.42), kind=kOutput, calls=%fused_computation.109.clone.1 | convolution fusion | flops 1107298304 | bytes 1591300 | tf_op jit(solution)/shard_map/while/body/eval_jaxpr/sub | solution.py:46
  156.1 12.2 %fusion.128 = bf16[4,1024,64]{1,2,0:T(8,128)(2,1)S(1)} fusion(bf16[2048,4,64]{0,2,1:T(8,128)(2,1)} %get-tuple-element.166, f32[4,1024]{1,0:T(4,128)S(1)} %fusion.127, pred[2048]{0:T(1024)(128)(4,1)S(1)} %iota_compare_fusion.3, bf16[2048,4,64]{0,2,1:T(8,128)(2,1)} %get-tuple-element.165, bf16[2048,4,64]{0,2,1:T(8,128)(2,1)} %get-tuple-element.164, ...), kind=kOutput, calls=%fused_computation.11.clone.1 | convolution fusion | flops 2189694976 | bytes 3164164 | tf_op jit(solution)/shard_map/while/body/eval_jaxpr/hqk,khd->qhd/dot_general | solution.py:48
  168.3 0.2 copy.45
  168.5 0.8 constant_dynamic-update-slice_fusion.2
  169.3 0.0 copy-start.5
  169.3 0.0 copy-start.6
  169.3 3.6 %all-to-all-start.1 = ((bf16[4,512,256]{2,1,0:T(8,128)(2,1)}), bf16[4,512,256]{2,1,0:T(8,128)(2,1)S(1)}, u32[]{:S(2)}, u32[]{:S(2)}) async-start(bf16[4,512,256]{2,1,0:T(8,128)(2,1)} %bitcast.63), calls=%async_computation.1 | async-start | bytes 2097152 | tf_op jit(solution)/shard_map/all_to_all | solution.py:99
  173.6 0.0 copy-done.2
  173.6 0.1 multiply_reduce_fusion.3
  173.8 24.3 %all-to-all-done.1 = bf16[4,512,256]{2,1,0:T(8,128)(2,1)S(1)} async-done(((bf16[4,512,256]{2,1,0:T(8,128)(2,1)}), bf16[4,512,256]{2,1,0:T(8,128)(2,1)S(1)}, u32[]{:S(2)}, u32[]{:S(2)}) %all-to-all-start.1) | async-done | bytes 1048608 | tf_op jit(solution)/shard_map/all_to_all | solution.py:99
  198.1 1.3 copy.41
  199.4 0.0 copy-done
  199.4 2.9 %fusion.98 = (f32[512]{0:T(512)S(1)}, f32[512,1024]{1,0:T(8,128)S(1)}) fusion(bf16[1,512,1024]{2,1,0:T(8,128)(2,1)} %param.14, bf16[512,1024]{0,1:T(8,128)(2,1)} %bitcast.59, bf16[1024,1024]{1,0:T(8,128)(2,1)S(1)} %copy-done), kind=kOutput, calls=%fused_computation.111 | convolution fusion | flops 1075314176 | bytes 6293504 | tf_op jit(solution)/shard_map/dot_general | solution.py:100
  202.3 0.0 copy-start.1
  202.3 1.3 copy-done.1
  203.6 0.3 multiply_reduce_fusion.2
  204.0 0.0 copy-start.3
  204.0 0.0 copy-start.4
  204.0 0.0 copy-start.7
  204.0 0.0 all-gather.4.cloned.1.call-done
  204.1 0.0 all-gather.6.cloned.1.call-done
  204.1 0.0 copy-done.5
  204.1 0.0 copy-done.6
  204.1 33.2 %fusion.99 = (f32[512]{0:T(512)S(1)}, f32[512,1024]{1,0:T(8,128)}) fusion(f32[1024]{0:T(1024)S(1)} %copy-done.5, f32[1024]{0:T(1024)S(1)} %copy-done.6, f32[512]{0:T(512)S(1)} %add_rsqrt_fusion.1, f32[512,1024]{1,0:T(8,128)} %copy-done.1, f32[512]{0:T(512)S(1)} %broadcast_multiply_fusion.1, bf16[1024,4096]{1,0:T(8,128)(2,1)} %all-gather.6.cloned.1.call-done, ...), kind=kOutput, calls=%fused_computation.112 | convolution fusion | flops 8733065216 | bytes 20985856 | tf_op jit(solution)/shard_map/dot_general | solution.py:69
  237.3 1.9 multiply_reduce_fusion.1
  239.2 0.0 copy-done.3
  239.3 0.0 copy-done.4
  239.3 3.1 %multiply_reduce_fusion = (f32[1024]{0:T(1024)S(1)}, bf16[1,512,1024]{2,1,0:T(8,128)(2,1)}) fusion(f32[512,1024]{1,0:T(8,128)} %get-tuple-element.95, f32[512]{0:T(512)S(1)} %fusion.59, f32[1024]{0:T(1024)S(1)} %copy-done.3, f32[1024]{0:T(1024)S(1)} %copy-done.4, f32[512]{0:T(512)S(1)} %add_rsqrt_fusion, f32[512]{0:T(512)S(1)} %broadcast_multiply_fusion), kind=kLoop, calls=%fused_computation.47 | loop fusion | flops 3668992 | bytes 3164160 | tf_op jit(solution)/shard_map/reduce_sum | solution.py:109
  242.4 9.8 %psum.7 = f32[1024]{0:T(1024)S(1)} all-reduce(f32[1024]{0:T(1024)S(1)} %get-tuple-element.90), channel_id=1, replica_groups=mesh['seq'=4,'grp'=8] {'seq'}, use_global_device_ids=true, to_apply=%region_9.10 | all-reduce | flops 1024 | bytes 8192 | tf_op jit(solution)/shard_map/psum | solution.py:110
  252.1 0.6 multiply_reduce_fusion.4
  253.4 0.6 fusion.91
  254.0 8.9 %all-gather = bf16[8192]{0:T(1024)(128)(2,1)S(1)} all-gather(bf16[1024]{0:T(1024)(128)(2,1)S(1)} %get-tuple-element.81), channel_id=2, replica_groups=mesh['seq'=4,'grp'=8] {'grp'}, dimensions={0}, use_global_device_ids=true | all-gather | bytes 18432 | tf_op jit(solution)/shard_map/all_gather | solution.py:113
  262.9 0.0 copy-done.7
  262.9 0.2 exponential_reduce_fusion
  263.2 0.5 log_subtract_fusion
  (9 shorter events, 0.1 us)
Async XLA Ops:
  7.2 192.2 %copy-start = (bf16[1024,1024]{1,0:T(8,128)(2,1)S(1)}, bf16[1024,1024]{1,0:T(8,128)(2,1)}, u32[]{:S(2)}) copy-start(bf16[1024,1024]{1,0:T(8,128)(2,1)} %param.17) | copy-start | bytes 6291460
  7.2 196.9 %all-gather.4.cloned.1.call-start = ((), (), s32[]{:S(2)}) async-start(), calls=%async_computation.2 | async-start | bytes 9437184 | tf_op jit(solution)/shard_map/all_gather | solution.py:57
  7.9 196.2 %all-gather.6.cloned.1.call-start = ((), (), s32[]{:S(2)}) async-start(), calls=%async_computation.3 | async-start | bytes 9437184 | tf_op jit(solution)/shard_map/all_gather | solution.py:58
  25.7 77.2 %all-to-all-start = ((bf16[4,512,3,256]{1,3,2,0:T(8,128)(2,1)}), bf16[4,512,3,256]{1,3,2,0:T(8,128)(2,1)}, u32[]{:S(2)}, u32[]{:S(2)}) async-start(bf16[4,512,3,256]{1,3,2,0:T(8,128)(2,1)} %pad_maximum_fusion), calls=%async_computation | async-start | bytes 6291456 | tf_op jit(solution)/shard_map/all_to_all | solution.py:13
  117.1 56.6 %copy-start.2 = (f32[8,1024]{1,0:T(8,128)S(1)}, f32[8,1024]{1,0:T(8,128)}, u32[]{:S(2)}) copy-start(f32[8,1024]{1,0:T(8,128)} %param.24) | copy-start | bytes 98308
  169.3 34.8 %copy-start.5 = (f32[1024]{0:T(1024)S(1)}, f32[1024]{0:T(1024)}, u32[]{:S(2)}) copy-start(f32[1024]{0:T(1024)} %param.19) | copy-start | bytes 12292
  169.3 34.8 %copy-start.6 = (f32[1024]{0:T(1024)S(1)}, f32[1024]{0:T(1024)}, u32[]{:S(2)}) copy-start(f32[1024]{0:T(1024)} %param.18) | copy-start | bytes 12292
  169.3 28.8 %all-to-all-start.1 = ((bf16[4,512,256]{2,1,0:T(8,128)(2,1)}), bf16[4,512,256]{2,1,0:T(8,128)(2,1)S(1)}, u32[]{:S(2)}, u32[]{:S(2)}) async-start(bf16[4,512,256]{2,1,0:T(8,128)(2,1)} %bitcast.63), calls=%async_computation.1 | async-start | bytes 2097152 | tf_op jit(solution)/shard_map/all_to_all | solution.py:99
  202.3 1.4 copy-start.1
  204.0 35.3 %copy-start.3 = (f32[1024]{0:T(1024)S(1)}, f32[1024]{0:T(1024)}, u32[]{:S(2)}) copy-start(f32[1024]{0:T(1024)} %param.23) | copy-start | bytes 12292
  204.0 35.3 %copy-start.4 = (f32[1024]{0:T(1024)S(1)}, f32[1024]{0:T(1024)}, u32[]{:S(2)}) copy-start(f32[1024]{0:T(1024)} %param.22) | copy-start | bytes 12292
  204.0 58.9 %copy-start.7 = (s32[8]{0:T(128)S(1)}, s32[8]{0:T(128)}, u32[]{:S(2)}) copy-start(s32[8]{0:T(128)} %param.25) | copy-start | bytes 100
Sparse Core Ops, SparseCore 0:
  9.9 56.9 all-gather.3
  68.8 54.2 all-gather.5
